TPU v7x, 32 devices: a whole 2x2x4 slice. The times are simulated.
32 devices in a mesh: gx: 8 (over y, x, core), gy: 4 (over z).
Axes of the slice: x: 2, y: 2, z: 4, core: 2. Of those that a mesh axis runs over, the one named last changes fastest.
Arguments:
- volts: float32 [32, 4, 64, 512], P(None, None, 'gx', 'gy'), may hold values from -6 to 6
- cap: float32 [4, 64, 512], P(None, 'gx', 'gy'), may hold values from 0.05 to 1
- cond_x: float32 [4, 64, 512], P(None, 'gx', 'gy'), may hold values from 0.5 to 2
- cond_y: float32 [4, 64, 512], P(None, 'gx', 'gy'), may hold values from 0.5 to 2
- via: float32 [4, 64, 512], P(None, 'gx', 'gy'), may hold values from 0.2 to 2
- waveforms: float32 [64, 64], replicated, may hold values from -6 to 6
- placement: int32 [262144, 1], P(('gx', 'gy')), may hold values from 0 to 31; in each aligned block of 8192 rows (0 to 8191, 8192 to 16383, ...) at most 512 rows name the same one
- cells: int32 [262144], P(('gx', 'gy')), may hold values from 0 to 1023
- wave_ids: int32 [262144], P(('gx', 'gy')), may hold values from 0 to 63
- amps: float32 [262144], P(('gx', 'gy')), may hold values from 0.5 to 4
Outputs:
- volts_out: float32 [32, 4, 64, 512], P(None, None, 'gx', 'gy')
- residual: float32 [32, 4, 64, 512], P(None, None, 'gx', 'gy')
Inputs may be any that keep to these rules, and one draw needn't show every extreme that they name: `placement`: in each device's block of 8192 rows no tile is named more than 512 times, a bound that some block reaches.
All inputs are finite; a program needn't handle non-finite values.
Results may differ from a plain program's by a relative error of at most 0.0029.
Values may be sent and summed in bfloat16 or wider, within the bound.
A program may use at most 64 MiB of HBM per device.

v0:
```python
import jax
import jax.numpy as jnp
from jax import lax
from jax.sharding import PartitionSpec as P

ITERS = 3


def with_halo(block, sides, width):
    for axis, dim in sides:
        count = lax.axis_size(axis)
        forward = [(i, i + 1) for i in range(count - 1)]
        backward = [(target, source) for source, target in forward]
        low = lax.ppermute(
            lax.slice_in_dim(block, block.shape[dim] - width, None, axis=dim), axis, forward
        )
        high = lax.ppermute(lax.slice_in_dim(block, 0, width, axis=dim), axis, backward)
        block = jnp.concatenate([low, block, high], axis=dim)
    return block


def shifted(x, axis, by):
    length = lax.axis_size(axis)
    pairs = [(i, i + by) for i in range(length) if 0 <= i + by < length]
    return lax.ppermute(x, axis, pairs)


def gram(left, right):
    left_rows = left.reshape(left.shape[0], -1)
    right_rows = right.reshape(right.shape[0], -1)
    return lax.dot_general(
        left_rows, right_rows, (((1,), (1,)), ((), ())), precision=lax.Precision.HIGHEST
    )


def combine(coef, field):
    return jnp.einsum("st,slxy->tlxy", coef, field, precision=lax.Precision.HIGHEST)


def spd_solve(matrix, right):
    factor = jnp.linalg.cholesky(matrix)
    return jax.scipy.linalg.cho_solve((factor, True), right)


def make_currents(waveforms, kinds, scales):
    table_hits = (
        jnp.arange(waveforms.shape[1], dtype=jnp.int32)[:, None] == kinds[None, :]
    ).astype(jnp.float32)
    picked = jnp.dot(waveforms, table_hits, precision=lax.Precision.HIGHEST)
    return (picked * scales[None, :]).astype(jnp.bfloat16)


def operate(field, cap, cond_x, cond_x_low, cond_y, cond_y_low, via, via_low):
    padded = with_halo(field, (("gx", 2), ("gy", 3)), 1)
    zero_layer = jnp.zeros_like(field[:, :1])
    upper = jnp.concatenate([field[:, 1:], zero_layer], axis=1)
    lower = jnp.concatenate([zero_layer, field[:, :-1]], axis=1)
    result = cap * field
    result = result + cond_x * (field - padded[:, :, 2:, 1:-1])
    result = result + cond_x_low * (field - padded[:, :, :-2, 1:-1])
    result = result + cond_y * (field - padded[:, :, 1:-1, 2:])
    result = result + cond_y_low * (field - padded[:, :, 1:-1, :-2])
    result = result + via * (field - upper) + via_low * (field - lower)
    return result


def body(volts, cap, cond_x, cond_y, via, waveforms, placement, cells, wave_ids, amps):
    devices = lax.axis_size(("gx", "gy"))
    scenarios = volts.shape[0]
    steps = waveforms.shape[0] // scenarios
    tile_x = volts.shape[2]
    tile_y = volts.shape[3]
    die_cells = tile_x * tile_y
    slots_all = 2 * cells.shape[0]
    capacity = slots_all // devices
    target = placement[:, 0]
    target_hits = (jnp.arange(devices, dtype=jnp.int32)[:, None] == target[None, :]).astype(
        jnp.int32
    )
    running = jnp.cumsum(target_hits, axis=1) - 1
    position = jnp.sum(target_hits * running, axis=0)
    slot_index = target * capacity + position
    currents = make_currents(waveforms, wave_ids, amps)
    packed = jnp.zeros((currents.shape[0], slots_all), jnp.bfloat16).at[:, slot_index].set(currents)
    cell_slots = jnp.zeros((1, slots_all), jnp.int32).at[0, slot_index].set(cells)
    arrived, cell_slots = (
        lax.all_to_all(packed, ("gx", "gy"), split_axis=1, concat_axis=1, tiled=True),
        lax.all_to_all(cell_slots, ("gx", "gy"), split_axis=1, concat_axis=1, tiled=True),
    )
    block_rows = min(1024, slots_all)
    block_count = slots_all // block_rows
    cell_line = jnp.arange(die_cells, dtype=jnp.int32)

    def add_block(turn, total):
        piece_values = lax.dynamic_slice_in_dim(arrived, turn * block_rows, block_rows, 1)
        piece_cells = lax.dynamic_slice_in_dim(cell_slots[0], turn * block_rows, block_rows, 0)
        one_hot = (piece_cells[:, None] == cell_line[None, :]).astype(jnp.bfloat16)
        return total + jnp.dot(piece_values, one_hot, preferred_element_type=jnp.float32)

    injected = lax.fori_loop(
        0, block_count, add_block, jnp.zeros((arrived.shape[0], die_cells), jnp.float32)
    )
    injected = injected.reshape(steps, scenarios, tile_x, tile_y)
    rim_x = shifted(cond_x[:, -1:, :], "gx", 1)
    rim_y = shifted(cond_y[:, :, -1:], "gy", 1)
    cond_x_low = jnp.concatenate([rim_x, cond_x[:, :-1, :]], axis=1)
    cond_y_low = jnp.concatenate([rim_y, cond_y[:, :, :-1]], axis=2)
    via_low = jnp.concatenate([jnp.zeros_like(via[:1]), via[:-1]], axis=0)

    def apply_grid(field):
        return operate(field, cap, cond_x, cond_x_low, cond_y, cond_y_low, via, via_low)

    voltage = volts
    residual = volts
    for step in range(steps):
        rhs = cap * voltage
        rhs = rhs.at[:, 0].add(-injected[step])
        iterate = voltage
        residual = rhs - apply_grid(iterate)
        direction = residual
        norm_gram = lax.psum(gram(residual, residual), ("gx", "gy"))
        for sweep in range(ITERS):
            image = apply_grid(direction)
            curve_gram, cross_gram, image_gram = lax.psum(
                (gram(direction, image), gram(residual, image), gram(image, image)), ("gx", "gy")
            )
            step_coef = spd_solve(curve_gram, norm_gram)
            iterate = iterate + combine(step_coef, direction)
            residual = residual - combine(step_coef, image)
            if sweep + 1 < ITERS:
                cross_term = jnp.dot(cross_gram, step_coef, precision=lax.Precision.HIGHEST)
                square_term = jnp.dot(
                    step_coef.T,
                    jnp.dot(image_gram, step_coef, precision=lax.Precision.HIGHEST),
                    precision=lax.Precision.HIGHEST,
                )
                new_gram = norm_gram - cross_term - cross_term.T + square_term
                turn_coef = spd_solve(norm_gram, new_gram)
                direction = residual + combine(turn_coef, direction)
                norm_gram = new_gram
        voltage = iterate
    return (voltage, residual)


def solution(mesh):
    return jax.shard_map(
        body,
        mesh=mesh,
        in_specs=(
            P(None, None, "gx", "gy"),
            P(None, "gx", "gy"),
            P(None, "gx", "gy"),
            P(None, "gx", "gy"),
            P(None, "gx", "gy"),
            P(),
            P(("gx", "gy"), None),
            P(("gx", "gy")),
            P(("gx", "gy")),
            P(("gx", "gy")),
        ),
        out_specs=(P(None, None, "gx", "gy"), P(None, None, "gx", "gy")),
        check_vma=False,
    )
```

profile of v0, /device:TPU:0, one launch (start us, length us, event | category | flops | bytes accessed | tf_op | source)
XLA Modules:
  0.0 647.4 jit_solution(1546838298687216187)
XLA Ops:
  1.6 9.5 %reduce-window.6 = s32[32,64,128]{2,1,0:T(8,128)S(1)} reduce-window(s32[32,64,128]{2,1,0:T(8,128)S(1)} %fusion.11, s32[]{:T(128)} %constant.128.clone.1), window={size=1x1x128 pad=0_0x0_0x127_0}, to_apply=%region_0.0 | reduce-window | flops 33292288 | bytes 2097156 | tf_op jit(solution)/shard_map/reduce-window
  14.9 23.7 %scatter_custom_fusion = bf16[64,16384]{0,1:T(8,128)(2,1)} fusion(s32[8192]{0:T(1024)S(1)} %bitcast.343, bf16[8192,64]{1,0:T(8,128)(2,1)S(1)} %copy.219, bf16[]{:T(256)} %constant.130.clone.1), kind=kCustom, calls=%fused_computation.13 | custom fusion | bytes 2097154 | tf_op jit(solution)/shard_map/scatter | solution.py:84
  38.6 4.8 copy.220
  43.3 7.3 %all-to-all-start = ((bf16[64,32,512]{2,0,1:T(8,128)(2,1)}), bf16[64,32,512]{2,0,1:T(8,128)(2,1)S(1)}, u32[]{:S(2)}, u32[]{:S(2)}) async-start(bf16[64,32,512]{2,0,1:T(8,128)(2,1)} %copy.220), calls=%async_computation | async-start | bytes 4194304 | tf_op jit(solution)/shard_map/all_to_all | solution.py:87
  55.2 3.5 collective-permute-start.4
  58.8 3.7 collective-permute-start.1
  62.9 31.2 %scatter_custom_fusion.1 = s32[16384]{0:T(1024)} fusion(s32[8192]{0:T(1024)S(1)} %broadcast_select_fusion, s32[8192]{0:T(1024)} %param.26, s32[]{:T(128)} %constant.128.clone.1), kind=kCustom, calls=%fused_computation.270 | custom fusion | bytes 66048
  97.6 7.3 %all-to-all-start.1 = ((s32[1,32,512]{2,0,1:T(1,128)}), s32[1,32,512]{2,0,1:T(1,128)}, u32[]{:S(2)}, u32[]{:S(2)}) async-start(s32[1,32,512]{2,0,1:T(1,128)} %bitcast.344), calls=%async_computation.1 | async-start | bytes 131072 | tf_op jit(solution)/shard_map/all_to_all | solution.py:88
  110.3 4.7 collective-permute-start.5
  119.0 53.7 %while.16 = (s32[]{:T(128)}, f32[64,1024]{1,0:T(8,128)}, bf16[64,16384]{1,0:T(8,128)(2,1)}, s32[1,16384]{1,0:T(1,128)}, s32[]{:T(128)}, /*index=5*/s32[]{:T(128)}, s32[]{:T(128)}, s32[]{:T(128)}) while((s32[]{:T(128)}, f32[64,1024]{1,0:T(8,128)}, bf16[64,16384]{1,0:T(8,128)(2,1)}, s32[1,16384]{1,0:T(1,128)}, s32[]{:T(128)}, ...), condition=%wide.region_6.7_spmd.clone, body=%wide.region_5.6_spmd.clone.sunk | while | flops 135397376 | bytes 667797 | solution.py:100
  119.8 2.6 fusion.346
  123.1 2.7 fusion.346
  126.4 2.7 fusion.346
  129.8 2.7 fusion.346
  133.1 2.7 fusion.346
  136.5 2.7 fusion.346
  139.8 2.7 fusion.346
  143.2 2.7 fusion.346
  146.5 2.7 fusion.346
  149.9 2.7 fusion.346
  153.3 2.7 fusion.346
  156.6 2.7 fusion.346
  160.0 2.7 fusion.346
  163.3 2.7 fusion.346
  166.7 2.7 fusion.346
  170.1 2.7 fusion.346
  177.6 3.0 collective-permute-start.7
  183.8 4.8 collective-permute-start.9
  192.3 44.5 %all-reduce.21 = (f32[32,32]{0,1:T(8,128)S(1)}, f32[32,32]{0,1:T(8,128)S(1)}, f32[32,32]{1,0:T(8,128)S(1)}) all-reduce(f32[32,32]{0,1:T(8,128)S(1)} %convolution_bitcast_fusion.18, f32[32,32]{0,1:T(8,128)S(1)} %convolution_bitcast_fusion.19, f32[32,32]{1,0:T(8,128)S(1)} %convolution_bitcast_fusion.17), channel_id=1, replica_groups=mesh['gx'=8,'gy'=4] {'gx','gy'}, use_global_device_ids=true, to_apply=%region_10.12 | all-reduce | flops 3072 | bytes 24576 | tf_op jit(solution)/shard_map/psum | solution.py:121
  236.9 2.9 cholesky.164
  241.2 2.4 custom-call.17
  245.4 2.9 cholesky.175
  249.6 2.4 custom-call.18
  255.0 2.9 cholesky.197
  259.2 3.0 collective-permute-start.11
  266.5 4.8 collective-permute-start.13
  271.9 3.1 custom-call.20
  279.1 43.3 %all-reduce.20 = (f32[32,32]{0,1:T(8,128)S(1)}, f32[32,32]{1,0:T(8,128)S(1)}, f32[32,32]{1,0:T(8,128)S(1)}) all-reduce(f32[32,32]{0,1:T(8,128)S(1)} %convolution_bitcast_fusion.15, f32[32,32]{1,0:T(8,128)S(1)} %convolution_bitcast_fusion.13, f32[32,32]{1,0:T(8,128)S(1)} %convolution_bitcast_fusion.14), channel_id=1, replica_groups=mesh['gx'=8,'gy'=4] {'gx','gy'}, use_global_device_ids=true, to_apply=%region_12.15 | all-reduce | flops 3072 | bytes 24576 | tf_op jit(solution)/shard_map/psum | solution.py:124
  322.6 2.9 cholesky.186
  326.8 2.4 custom-call.19
  333.2 3.0 collective-permute-start.15
  340.4 4.5 collective-permute-start.17
  347.8 43.9 %psum.110 = f32[32,32]{0,1:T(8,128)S(1)} all-reduce(f32[32,32]{0,1:T(8,128)S(1)} %convolution_bitcast_fusion.11), channel_id=1, replica_groups=mesh['gx'=8,'gy'=4] {'gx','gy'}, use_global_device_ids=true, to_apply=%region_15.18 | all-reduce | flops 1024 | bytes 8192 | tf_op jit(solution)/shard_map/psum | solution.py:124
  391.7 2.9 cholesky.208
  395.9 2.4 custom-call.21
  400.8 3.0 collective-permute-start.19
  408.1 5.0 collective-permute-start.21
  417.5 3.3 collective-permute-start.23
  425.1 4.6 collective-permute-start.25
  434.3 46.8 %all-reduce.19 = (f32[32,32]{0,1:T(8,128)S(1)}, f32[32,32]{0,1:T(8,128)S(1)}, f32[32,32]{1,0:T(8,128)S(1)}) all-reduce(f32[32,32]{0,1:T(8,128)S(1)} %convolution_bitcast_fusion.8, f32[32,32]{0,1:T(8,128)S(1)} %convolution_bitcast_fusion.9, f32[32,32]{1,0:T(8,128)S(1)} %convolution_bitcast_fusion.7), channel_id=1, replica_groups=mesh['gx'=8,'gy'=4] {'gx','gy'}, use_global_device_ids=true, to_apply=%region_17.20 | all-reduce | flops 3072 | bytes 24576 | tf_op jit(solution)/shard_map/psum | solution.py:121
  481.2 2.9 cholesky.219
  485.5 2.4 custom-call.22
  489.7 2.9 cholesky.230
  499.9 2.9 cholesky.252
  504.1 3.0 collective-permute-start.27
  510.3 4.7 collective-permute-start.29
  515.7 3.1 custom-call.25
  522.7 42.7 %all-reduce.18 = (f32[32,32]{0,1:T(8,128)S(1)}, f32[32,32]{1,0:T(8,128)S(1)}, f32[32,32]{1,0:T(8,128)S(1)}) all-reduce(f32[32,32]{0,1:T(8,128)S(1)} %convolution_bitcast_fusion.5, f32[32,32]{1,0:T(8,128)S(1)} %convolution_bitcast_fusion.3, f32[32,32]{1,0:T(8,128)S(1)} %convolution_bitcast_fusion.4), channel_id=1, replica_groups=mesh['gx'=8,'gy'=4] {'gx','gy'}, use_global_device_ids=true, to_apply=%region_19.22 | all-reduce | flops 3072 | bytes 24576 | tf_op jit(solution)/shard_map/psum | solution.py:124
  565.5 2.9 cholesky.241
  576.2 3.0 collective-permute-start.31
  583.3 4.5 collective-permute-start.33
  592.0 44.5 %psum.117 = f32[32,32]{0,1:T(8,128)S(1)} all-reduce(f32[32,32]{0,1:T(8,128)S(1)} %convolution_bitcast_fusion.1), channel_id=1, replica_groups=mesh['gx'=8,'gy'=4] {'gx','gy'}, use_global_device_ids=true, to_apply=%region_22.25 | all-reduce | flops 1024 | bytes 8192 | tf_op jit(solution)/shard_map/psum | solution.py:124
  636.6 2.9 cholesky.263
  640.9 2.4 custom-call.26
  (357 shorter events, 136.4 us)
Async XLA Ops:
  0.6 12.1 %copy-start = (f32[64,64]{1,0:T(8,128)S(1)}, f32[64,64]{1,0:T(8,128)}, u32[]{:S(2)}) copy-start(f32[64,64]{1,0:T(8,128)} %param.24) | copy-start | bytes 49156
  0.6 11.6 %copy-start.15 = (s32[8192,1]{0,1:T(1,128)S(1)}, s32[8192,1]{0,1:T(1,128)}, u32[]{:S(2)}) copy-start(s32[8192,1]{0,1:T(1,128)} %param.25) | copy-start | bytes 98308
  1.6 11.1 %copy-start.34 = (f32[8192]{0:T(1024)S(1)}, f32[8192]{0:T(1024)}, u32[]{:S(2)}) copy-start(f32[8192]{0:T(1024)} %param.28) | copy-start | bytes 98308
  1.6 11.1 %copy-start.35 = (s32[8192]{0:T(1024)S(1)}, s32[8192]{0:T(1024)}, u32[]{:S(2)}) copy-start(s32[8192]{0:T(1024)} %param.27) | copy-start | bytes 98308
  43.3 7.4 %copy-start.2 = (f32[32,4,8,128]{3,2,1,0:T(8,128)S(1)}, f32[32,4,8,128]{3,2,1,0:T(8,128)}, u32[]{:S(2)}) copy-start(f32[32,4,8,128]{3,2,1,0:T(8,128)} %param.19) | copy-start | bytes 1572868
  43.3 11.8 %copy-start.10 = (f32[4,8,128]{2,1,0:T(8,128)S(1)}, f32[4,8,128]{2,1,0:T(8,128)}, u32[]{:S(2)}) copy-start(f32[4,8,128]{2,1,0:T(8,128)} %param.22) | copy-start | bytes 49156
  43.3 15.4 %copy-start.11 = (f32[4,8,128]{2,1,0:T(8,128)S(1)}, f32[4,8,128]{2,1,0:T(8,128)}, u32[]{:S(2)}) copy-start(f32[4,8,128]{2,1,0:T(8,128)} %param.21) | copy-start | bytes 49156
  43.3 19.2 %copy-start.32 = (s32[2]{0:T(128)S(1)}, s32[2]{0:T(128)}, u32[]{:S(2)}) copy-start(s32[2]{0:T(128)} %constant.170) | copy-start | bytes 28
  43.3 19.3 %copy-start.33 = (s32[2]{0:T(128)S(1)}, s32[2]{0:T(128)}, u32[]{:S(2)}) copy-start(s32[2]{0:T(128)} %constant.173) | copy-start | bytes 28
  43.3 54.2 %all-to-all-start = ((bf16[64,32,512]{2,0,1:T(8,128)(2,1)}), bf16[64,32,512]{2,0,1:T(8,128)(2,1)S(1)}, u32[]{:S(2)}, u32[]{:S(2)}) async-start(bf16[64,32,512]{2,0,1:T(8,128)(2,1)} %copy.220), calls=%async_computation | async-start | bytes 4194304 | tf_op jit(solution)/shard_map/all_to_all | solution.py:87
  50.7 44.4 %slice-start = ((f32[4,8,128]{2,1,0:T(8,128)}), f32[3,8,128]{2,1,0:T(8,128)S(1)}, s32[]{:S(2)}) async-start(f32[4,8,128]{2,1,0:T(8,128)} %param.23), calls=%async_computation.2 | async-start | bytes 24576 | tf_op jit(solution)/shard_map/slice | solution.py:108
  50.7 44.5 %copy-start.9 = (f32[4,8,128]{2,1,0:T(8,128)S(1)}, f32[4,8,128]{2,1,0:T(8,128)}, u32[]{:S(2)}) copy-start(f32[4,8,128]{2,1,0:T(8,128)} %param.20) | copy-start | bytes 49156
  51.7 43.5 %collective-permute-start.2 = (f32[32,4,1,128]{3,0,2,1:T(8,128)S(1)}, f32[32,4,1,128]{3,0,2,1:T(8,128)S(1)}, u32[]{:S(2)}, u32[]{:S(2)}) collective-permute-start(f32[32,4,1,128]{3,0,2,1:T(8,128)S(1)} %get-tuple-element.215), channel_id=1, source_target_pairs={{0,4},{4,8},{8,12},{12,16},{16,20},{20,24},{24,28},{1,5},{5,9},{9,... | collective-permute-start | bytes 196616 | tf_op jit(solution)/shard_map/ppermute | solution.py:14
  53.8 43.6 %collective-permute-start = (f32[32,4,1,128]{3,0,2,1:T(8,128)}, f32[32,4,1,128]{3,0,2,1:T(8,128)S(1)}, u32[]{:S(2)}, u32[]{:S(2)}) collective-permute-start(f32[32,4,1,128]{3,0,2,1:T(8,128)} %get-tuple-element.214), channel_id=1, source_target_pairs={{4,0},{8,4},{12,8},{16,12},{20,16},{24,20},{28,24},{5,1},{9,5},{13... | collective-permute-start | bytes 196616 | tf_op jit(solution)/shard_map/ppermute | solution.py:17
  55.2 39.9 %collective-permute-start.4 = (f32[4,8,1]{2,1,0:T(8,128)S(1)}, f32[4,8,1]{2,1,0:T(8,128)S(1)}, u32[]{:S(2)}, u32[]{:S(2)}) collective-permute-start(f32[4,8,1]{2,1,0:T(8,128)S(1)} %slice.379), channel_id=1, source_target_pairs={{0,1},{1,2},{2,3},{4,5},{5,6},{6,7},{8,9},{9,10},{10,11},{12,13},{... | collective-permute-start | bytes 392 | tf_op jit(solution)/shard_map/ppermute | solution.py:25
  58.8 56.2 %collective-permute-start.1 = (f32[4,1,128]{2,1,0:T(1,128)S(1)}, f32[4,1,128]{2,1,0:T(1,128)S(1)}, u32[]{:S(2)}, u32[]{:S(2)}) collective-permute-start(f32[4,1,128]{2,1,0:T(1,128)S(1)} %slice.373), channel_id=1, source_target_pairs={{0,4},{4,8},{8,12},{12,16},{16,20},{20,24},{24,28},{1,5},{5,9},{9,... | collective-permute-start | bytes 6152 | tf_op jit(solution)/shard_map/ppermute | solution.py:25
  95.2 11.0 %copy-start.18 = (f32[32,4,1,128]{3,0,2,1:T(8,128)}, f32[32,4,1,128]{3,0,2,1:T(8,128)S(1)}, u32[]{:S(2)}) copy-start(f32[32,4,1,128]{3,0,2,1:T(8,128)S(1)} %collective-permute-done.2) | copy-start | bytes 196612
  97.4 12.9 %copy-start.19 = (f32[32,4,1,128]{3,0,2,1:T(8,128)}, f32[32,4,1,128]{3,0,2,1:T(8,128)S(1)}, u32[]{:S(2)}) copy-start(f32[32,4,1,128]{3,0,2,1:T(8,128)S(1)} %collective-permute-done) | copy-start | bytes 196612
  97.6 21.4 %all-to-all-start.1 = ((s32[1,32,512]{2,0,1:T(1,128)}), s32[1,32,512]{2,0,1:T(1,128)}, u32[]{:S(2)}, u32[]{:S(2)}) async-start(s32[1,32,512]{2,0,1:T(1,128)} %bitcast.344), calls=%async_computation.1 | async-start | bytes 131072 | tf_op jit(solution)/shard_map/all_to_all | solution.py:88
  107.6 7.4 %collective-permute-start.3 = (f32[32,4,10,1]{0,1,3,2:T(4,128)S(1)}, f32[32,4,10,1]{0,1,3,2:T(4,128)S(1)}, u32[]{:S(2)}, u32[]{:S(2)}) collective-permute-start(f32[32,4,10,1]{0,1,3,2:T(4,128)S(1)} %copy.230), channel_id=1, source_target_pairs={{1,0},{2,1},{3,2},{5,4},{6,5},{7,6},{9,8},{10,9},{11,10},{13,12},{... | collective-permute-start | bytes 15368 | tf_op jit(solution)/shard_map/ppermute | solution.py:17
  110.3 6.0 collective-permute-start.5
  119.0 55.4 %copy-start.4 = (f32[32,4,8,128]{3,0,2,1:T(8,128)S(1)}, f32[32,4,8,128]{3,0,2,1:T(8,128)}, u32[]{:S(2)}) copy-start(f32[32,4,8,128]{3,0,2,1:T(8,128)} %get-tuple-element.217) | copy-start | bytes 1572868
  119.0 55.5 %copy-start.5 = (f32[32,4,10,1]{3,0,2,1:T(8,128)S(1)}, f32[32,4,10,1]{3,0,2,1:T(8,128)}, u32[]{:S(2)}) copy-start(f32[32,4,10,1]{3,0,2,1:T(8,128)} %copy.231) | copy-start | bytes 15364
  119.0 55.5 %copy-start.7 = (f32[32,3,8,128]{3,0,2,1:T(8,128)S(1)}, f32[32,3,8,128]{3,0,2,1:T(8,128)}, u32[]{:S(2)}) copy-start(f32[32,3,8,128]{3,0,2,1:T(8,128)} %get-tuple-element.212) | copy-start | bytes 1179652
  119.0 55.5 %copy-start.12 = (f32[4,8,128]{2,1,0:T(8,128)S(1)}, f32[4,8,128]{2,1,0:T(8,128)}, u32[]{:S(2)}) copy-start(f32[4,8,128]{2,1,0:T(8,128)} %param.23) | copy-start | bytes 49156
  176.3 4.4 collective-permute-start.6
  177.6 3.9 collective-permute-start.7
  181.6 7.6 %copy-start.14 = (f32[4,8,8,128]{3,1,2,0:T(8,128)S(1)}, f32[4,8,8,128]{3,1,2,0:T(8,128)}, u32[]{:S(2)}) copy-start(f32[4,8,8,128]{3,1,2,0:T(8,128)} %get-tuple-element.218) | copy-start | bytes 393220
  182.2 7.7 %collective-permute-start.8 = (f32[32,4,10,1]{0,1,3,2:T(4,128)S(1)}, f32[32,4,10,1]{0,1,3,2:T(4,128)S(1)}, u32[]{:S(2)}, u32[]{:S(2)}) collective-permute-start(f32[32,4,10,1]{0,1,3,2:T(4,128)S(1)} %copy.240), channel_id=1, source_target_pairs={{1,0},{2,1},{3,2},{5,4},{6,5},{7,6},{9,8},{10,9},{11,10},{13,12},{... | collective-permute-start | bytes 15368 | tf_op jit(solution)/shard_map/ppermute | solution.py:17
  183.8 6.4 collective-permute-start.9
  244.9 9.3 %copy-start.3 = (f32[32,4,8,128]{3,2,1,0:T(8,128)S(1)}, f32[32,4,8,128]{3,2,1,0:T(8,128)}, u32[]{:S(2)}) copy-start(f32[32,4,8,128]{3,2,1,0:T(8,128)} %param.19) | copy-start | bytes 1572868
  257.9 5.1 collective-permute-start.10
  259.2 3.9 collective-permute-start.11
  264.9 10.1 %collective-permute-start.12 = (f32[32,4,10,1]{0,1,3,2:T(4,128)S(1)}, f32[32,4,10,1]{0,1,3,2:T(4,128)S(1)}, u32[]{:S(2)}, u32[]{:S(2)}) collective-permute-start(f32[32,4,10,1]{0,1,3,2:T(4,128)S(1)} %copy.254), channel_id=1, source_target_pairs={{1,0},{2,1},{3,2},{5,4},{6,5},{7,6},{9,8},{10,9},{11,10},{13,12},{... | collective-permute-start | bytes 15368 | tf_op jit(solution)/shard_map/ppermute | solution.py:17
  266.5 8.9 %collective-permute-start.13 = (f32[32,4,10,1]{0,1,3,2:T(4,128)S(1)}, f32[32,4,10,1]{0,1,3,2:T(4,128)S(1)}, u32[]{:S(2)}, u32[]{:S(2)}) collective-permute-start(f32[32,4,10,1]{0,1,3,2:T(4,128)S(1)} %copy.256), channel_id=1, source_target_pairs={{0,1},{1,2},{2,3},{4,5},{5,6},{6,7},{8,9},{9,10},{10,11},{12,13},{... | collective-permute-start | bytes 15368 | tf_op jit(solution)/shard_map/ppermute | solution.py:14
  278.0 52.9 %copy-start.30 = (f32[1,32,32]{1,2,0:T(8,128)S(1)}, f32[1,32,32]{1,2,0:T(8,128)}, u32[]{:S(2)}) copy-start(f32[1,32,32]{1,2,0:T(8,128)} %custom-call.20) | copy-start | bytes 12292
  331.9 5.0 collective-permute-start.14
  333.2 3.9 collective-permute-start.15
  336.9 0.6 copy-start.26
  338.5 8.3 %copy-start.27 = (f32[32,4,1,128]{3,0,2,1:T(8,128)S(1)}, f32[32,4,1,128]{3,0,2,1:T(8,128)}, u32[]{:S(2)}) copy-start(f32[32,4,1,128]{3,0,2,1:T(8,128)} %copy-done.26) | copy-start | bytes 196612
  338.5 8.3 %copy-start.29 = (f32[32,4,1,128]{3,0,2,1:T(8,128)S(1)}, f32[32,4,1,128]{3,0,2,1:T(8,128)}, u32[]{:S(2)}) copy-start(f32[32,4,1,128]{3,0,2,1:T(8,128)} %copy-done.28) | copy-start | bytes 196612
  338.8 6.3 collective-permute-start.16
  340.4 6.0 collective-permute-start.17
  399.5 5.2 collective-permute-start.18
  400.8 3.9 collective-permute-start.19
  406.0 7.1 %copy-start.13 = (f32[4,8,8,128]{3,2,1,0:T(8,128)S(1)}, f32[4,8,8,128]{3,2,1,0:T(8,128)}, u32[]{:S(2)}) copy-start(f32[4,8,8,128]{3,2,1,0:T(8,128)} %copy.370) | copy-start | bytes 393220
  406.5 6.6 %collective-permute-start.20 = (f32[32,4,10,1]{0,1,3,2:T(4,128)S(1)}, f32[32,4,10,1]{0,1,3,2:T(4,128)S(1)}, u32[]{:S(2)}, u32[]{:S(2)}) collective-permute-start(f32[32,4,10,1]{0,1,3,2:T(4,128)S(1)} %copy.274), channel_id=1, source_target_pairs={{1,0},{2,1},{3,2},{5,4},{6,5},{7,6},{9,8},{10,9},{11,10},{13,12},{... | collective-permute-start | bytes 15368 | tf_op jit(solution)/shard_map/ppermute | solution.py:17
  408.1 6.0 collective-permute-start.21
  416.2 5.4 collective-permute-start.22
  417.5 4.2 collective-permute-start.23
  423.5 6.7 %collective-permute-start.24 = (f32[32,4,10,1]{0,1,3,2:T(4,128)S(1)}, f32[32,4,10,1]{0,1,3,2:T(4,128)S(1)}, u32[]{:S(2)}, u32[]{:S(2)}) collective-permute-start(f32[32,4,10,1]{0,1,3,2:T(4,128)S(1)} %copy.278), channel_id=1, source_target_pairs={{1,0},{2,1},{3,2},{5,4},{6,5},{7,6},{9,8},{10,9},{11,10},{13,12},{... | collective-permute-start | bytes 15368 | tf_op jit(solution)/shard_map/ppermute | solution.py:17
  425.1 6.0 collective-permute-start.25
  502.8 5.0 collective-permute-start.26
  504.1 3.9 collective-permute-start.27
  508.1 11.3 %copy-start.8 = (f32[32,3,8,128]{3,0,2,1:T(8,128)S(1)}, f32[32,3,8,128]{3,0,2,1:T(8,128)}, u32[]{:S(2)}) copy-start(f32[32,3,8,128]{3,0,2,1:T(8,128)} %get-tuple-element.188) | copy-start | bytes 1179652
  508.7 10.0 %collective-permute-start.28 = (f32[32,4,10,1]{0,1,3,2:T(4,128)S(1)}, f32[32,4,10,1]{0,1,3,2:T(4,128)S(1)}, u32[]{:S(2)}, u32[]{:S(2)}) collective-permute-start(f32[32,4,10,1]{0,1,3,2:T(4,128)S(1)} %copy.291), channel_id=1, source_target_pairs={{1,0},{2,1},{3,2},{5,4},{6,5},{7,6},{9,8},{10,9},{11,10},{13,12},{... | collective-permute-start | bytes 15368 | tf_op jit(solution)/shard_map/ppermute | solution.py:17
  510.3 8.8 %collective-permute-start.29 = (f32[32,4,10,1]{0,1,3,2:T(4,128)S(1)}, f32[32,4,10,1]{0,1,3,2:T(4,128)S(1)}, u32[]{:S(2)}, u32[]{:S(2)}) collective-permute-start(f32[32,4,10,1]{0,1,3,2:T(4,128)S(1)} %copy.293), channel_id=1, source_target_pairs={{0,1},{1,2},{2,3},{4,5},{5,6},{6,7},{8,9},{9,10},{10,11},{12,13},{... | collective-permute-start | bytes 15368 | tf_op jit(solution)/shard_map/ppermute | solution.py:14
  521.5 52.3 %copy-start.31 = (f32[1,32,32]{1,2,0:T(8,128)S(1)}, f32[1,32,32]{1,2,0:T(8,128)}, u32[]{:S(2)}) copy-start(f32[1,32,32]{1,2,0:T(8,128)} %custom-call.25) | copy-start | bytes 12292
  522.7 56.5 %copy-start.6 = (f32[32,4,8,128]{3,0,2,1:T(8,128)S(1)}, f32[32,4,8,128]{3,0,2,1:T(8,128)}, u32[]{:S(2)}) copy-start(f32[32,4,8,128]{3,0,2,1:T(8,128)} %convolution_add_fusion.4) | copy-start | bytes 1572868
  574.9 5.0 collective-permute-start.30
  576.2 3.9 collective-permute-start.31
  581.7 7.1 %collective-permute-start.32 = (f32[32,4,10,1]{0,1,3,2:T(4,128)S(1)}, f32[32,4,10,1]{0,1,3,2:T(4,128)S(1)}, u32[]{:S(2)}, u32[]{:S(2)}) collective-permute-start(f32[32,4,10,1]{0,1,3,2:T(4,128)S(1)} %copy.303), channel_id=1, source_target_pairs={{1,0},{2,1},{3,2},{5,4},{6,5},{7,6},{9,8},{10,9},{11,10},{13,12},{... | collective-permute-start | bytes 15368 | tf_op jit(solution)/shard_map/ppermute | solution.py:17
  583.3 6.0 collective-permute-start.33
  643.8 3.4 copy-start.1
  (9 other events, 5.6 us)
where the time goes:
time: 657 us; the launch traced here: 647 us
  blocking collectives  266 us (40%)
  local copies, waits for them, and re-layouts  107 us (16%)
  starting transfers between devices  104 us (16%)
  other arithmetic  95.1 us (14%)
  matrix products  68.5 us (10%)
    psum x4, blocking collectives, body(): lax.psum((gram(direction, image), gram(residual, image), gram(image, imag...  174 us
    psum x2, blocking collectives, body(): norm_gram = lax.psum(gram(residual, residual), ('gx', 'gy'))  91.3 us
    ppermute x16, starting transfers between devices, with_halo(): lax.ppermute(lax.slice_in_dim(block, block.shape[dim] - width, None, axis...  61.3 us
    dot_general x16, matrix products, add_block(): jnp.dot(piece_values, one_hot, preferred_element_type=jnp.float32)  42.7 us
    unnamed x79, local copies, waits for them, and re-layouts  40.2 us
    another operation x30, other arithmetic, spd_solve(): factor = jnp.linalg.cholesky(matrix)  36.1 us
    another operation x20, other arithmetic, spd_solve(): return jax.scipy.linalg.cho_solve((factor, True), right)  32.2 us
    scatter x1, local copies, waits for them, and re-layouts, body(): jnp.zeros((currents.shape[0], slots_all), jnp.bfloat16).at[:, slot_index]  23.7 us
  transfers between devices with their start and end apart: 36, of which 11 were waited for; matrix products, arithmetic and copies ran while one was open for 10% of the time, Pallas kernels for 0%

commit v1 on v0

--- a/solution.py
+++ b/solution.py
@@ -1,9 +1,19 @@
+import functools
 import jax
 import jax.numpy as jnp
 from jax import lax
 from jax.sharding import PartitionSpec as P
 
 ITERS = 3
+
+
+def find_lines(array_here, mesh_ax):
+    shaped = lax.all_gather(array_here, mesh_ax)
+    view_out = jnp.sum(shaped, axis=0)
+    return view_out
+
+
+obtain_the_roads = functools.partial(find_lines, mesh_ax=("gx", "gy"))
 
 
 def with_halo(block, sides, width):
@@ -118,7 +128,7 @@
         iterate = voltage
         residual = rhs - apply_grid(iterate)
         direction = residual
-        norm_gram = lax.psum(gram(residual, residual), ("gx", "gy"))
+        norm_gram = obtain_the_roads(gram(residual, residual))
         for sweep in range(ITERS):
             image = apply_grid(direction)
             curve_gram, cross_gram, image_gram = lax.psum(

time: 657 us -> 790 us (1.20)
  blocking collectives: 266 us -> 400 us
    all_gather x0 -> x2, blocking collectives: none -> 145 us  [find_lines(): shaped = lax.all_gather(array_here, mesh_ax)]
    psum x2 -> x0, blocking collectives: 91.3 us -> none  [body(): norm_gram = lax.psum(gram(residual, residual), ('gx', 'gy'))]
    psum x4 -> x6, blocking collectives: 174 us -> 254 us  [body(): lax.psum((gram(direction, image), gram(residual, image), gram(image, imag...]
    unnamed x79 -> x81, local copies, waits for them, and re-layouts: 40.2 us -> 38.9 us
  transfers between devices with their start and end apart: 36 -> 36, of which waited for: 11 -> 9; matrix products, arithmetic and copies ran while one was open for 10% -> 10% of each run, Pallas kernels for 0% -> 0%
where the time goes in v1:
time: 790 us; the launch traced here: 780 us
  blocking collectives  400 us (51%)
  local copies, waits for them, and re-layouts  106 us (13%)
  starting transfers between devices  104 us (13%)
  other arithmetic  96.5 us (12%)
  matrix products  68.6 us (9%)
    psum x6, blocking collectives, body(): lax.psum((gram(direction, image), gram(residual, image), gram(image, imag...  254 us
    all_gather x2, blocking collectives, find_lines(): shaped = lax.all_gather(array_here, mesh_ax)  145 us
    ppermute x16, starting transfers between devices, with_halo(): lax.ppermute(lax.slice_in_dim(block, block.shape[dim] - width, None, axis...  61 us
    dot_general x16, matrix products, add_block(): jnp.dot(piece_values, one_hot, preferred_element_type=jnp.float32)  42.9 us
    unnamed x81, local copies, waits for them, and re-layouts  38.9 us
    another operation x30, other arithmetic, spd_solve(): factor = jnp.linalg.cholesky(matrix)  36 us
    another operation x20, other arithmetic, spd_solve(): return jax.scipy.linalg.cho_solve((factor, True), right)  33.3 us
    scatter x1, local copies, waits for them, and re-layouts, body(): jnp.zeros((currents.shape[0], slots_all), jnp.bfloat16).at[:, slot_index]  23.7 us
  transfers between devices with their start and end apart: 36, of which 9 were waited for; matrix products, arithmetic and copies ran while one was open for 10% of the time, Pallas kernels for 0%

profile of v1, /device:TPU:0, one launch (start us, length us, event | category | flops | bytes accessed | tf_op | source)
XLA Modules:
  0.0 779.8 jit_solution(13002598303979023152)
XLA Ops:
  1.6 9.5 %reduce-window.6 = s32[32,64,128]{2,1,0:T(8,128)S(1)} reduce-window(s32[32,64,128]{2,1,0:T(8,128)S(1)} %fusion.11, s32[]{:T(128)} %constant.129.clone.1), window={size=1x1x128 pad=0_0x0_0x127_0}, to_apply=%region_0.0 | reduce-window | flops 33292288 | bytes 2097156 | tf_op jit(solution)/shard_map/reduce-window
  14.9 23.7 %scatter_custom_fusion = bf16[64,16384]{0,1:T(8,128)(2,1)} fusion(s32[8192]{0:T(1024)S(1)} %bitcast.351, bf16[8192,64]{1,0:T(8,128)(2,1)S(1)} %copy.215, bf16[]{:T(256)} %constant.131.clone.1), kind=kCustom, calls=%fused_computation.13 | custom fusion | bytes 2097154 | tf_op jit(solution)/shard_map/scatter | solution.py:94
  38.5 4.8 copy.216
  43.3 7.3 all-to-all-start
  55.2 3.5 collective-permute-start.4
  58.8 3.7 collective-permute-start.1
  62.9 31.2 %scatter_custom_fusion.1 = s32[16384]{0:T(1024)} fusion(s32[8192]{0:T(1024)S(1)} %broadcast_select_fusion, s32[8192]{0:T(1024)} %param.26, s32[]{:T(128)} %constant.129.clone.1), kind=kCustom, calls=%fused_computation.270 | custom fusion | bytes 66048
  97.6 7.3 all-to-all-start.1
  110.2 4.7 collective-permute-start.5
  119.0 53.9 %while.16 = (s32[]{:T(128)}, f32[64,1024]{1,0:T(8,128)}, bf16[64,16384]{1,0:T(8,128)(2,1)}, s32[1,16384]{1,0:T(1,128)}, s32[]{:T(128)}, /*index=5*/s32[]{:T(128)}, s32[]{:T(128)}, s32[]{:T(128)}) while((s32[]{:T(128)}, f32[64,1024]{1,0:T(8,128)}, bf16[64,16384]{1,0:T(8,128)(2,1)}, s32[1,16384]{1,0:T(1,128)}, s32[]{:T(128)}, ...), condition=%wide.region_6.7_spmd.clone, body=%wide.region_5.6_spmd.clone.sunk | while | flops 135397376 | bytes 667797 | solution.py:110
  119.8 2.6 fusion.346
  123.0 2.7 fusion.346
  126.4 2.7 fusion.346
  129.8 2.7 fusion.346
  133.1 2.7 fusion.346
  136.5 2.7 fusion.346
  139.9 2.7 fusion.346
  143.2 2.7 fusion.346
  146.6 2.7 fusion.346
  149.9 2.7 fusion.346
  153.3 2.7 fusion.346
  156.7 2.7 fusion.346
  160.1 2.7 fusion.346
  163.4 2.7 fusion.346
  166.8 2.7 fusion.346
  170.1 2.7 fusion.346
  178.4 3.0 collective-permute-start.7
  181.4 72.7 %all-gather = f32[1024,32]{1,0:T(8,128)S(1)} all-gather(f32[32,32]{1,0:T(8,128)S(1)} %convolution_bitcast_fusion.18), channel_id=2, replica_groups=mesh['gx'=8,'gy'=4] {'gx','gy'}, dimensions={0}, use_global_device_ids=true | all-gather | bytes 135168 | tf_op jit(solution)/shard_map/all_gather | solution.py:11
  254.3 2.9 cholesky.175
  260.1 4.5 collective-permute-start.9
  265.3 3.1 custom-call.18
  271.5 38.5 %all-reduce.21 = (f32[32,32]{0,1:T(8,128)S(1)}, f32[32,32]{1,0:T(8,128)S(1)}) all-reduce(f32[32,32]{0,1:T(8,128)S(1)} %convolution_bitcast_fusion.19, f32[32,32]{1,0:T(8,128)S(1)} %convolution_bitcast_fusion.17), channel_id=1, replica_groups=mesh['gx'=8,'gy'=4] {'gx','gy'}, use_global_device_ids=true, to_apply=%region_7.8 | all-reduce | flops 2048 | bytes 16384 | tf_op jit(solution)/shard_map/psum | solution.py:134
  310.1 2.9 cholesky.164
  314.4 2.4 custom-call.17
  321.5 2.9 cholesky.197
  325.7 3.0 collective-permute-start.11
  332.9 4.8 collective-permute-start.13
  338.4 3.1 custom-call.20
  345.6 44.2 %all-reduce.20 = (f32[32,32]{0,1:T(8,128)S(1)}, f32[32,32]{1,0:T(8,128)S(1)}, f32[32,32]{1,0:T(8,128)S(1)}) all-reduce(f32[32,32]{0,1:T(8,128)S(1)} %convolution_bitcast_fusion.15, f32[32,32]{1,0:T(8,128)S(1)} %convolution_bitcast_fusion.13, f32[32,32]{1,0:T(8,128)S(1)} %convolution_bitcast_fusion.14), channel_id=1, replica_groups=mesh['gx'=8,'gy'=4] {'gx','gy'}, use_global_device_ids=true, to_apply=%region_12.15 | all-reduce | flops 3072 | bytes 24576 | tf_op jit(solution)/shard_map/psum | solution.py:134
  389.9 2.9 cholesky.186
  394.2 2.4 custom-call.19
  400.6 3.0 collective-permute-start.15
  407.8 4.5 collective-permute-start.17
  415.1 43.8 %psum.95 = f32[32,32]{0,1:T(8,128)S(1)} all-reduce(f32[32,32]{0,1:T(8,128)S(1)} %convolution_bitcast_fusion.11), channel_id=1, replica_groups=mesh['gx'=8,'gy'=4] {'gx','gy'}, use_global_device_ids=true, to_apply=%region_15.18 | all-reduce | flops 1024 | bytes 8192 | tf_op jit(solution)/shard_map/psum | solution.py:134
  459.0 2.9 cholesky.208
  468.0 3.0 collective-permute-start.19
  475.4 5.0 collective-permute-start.21
  486.2 3.3 collective-permute-start.23
  489.5 72.6 %all-gather.1 = f32[1024,32]{1,0:T(8,128)S(1)} all-gather(f32[32,32]{1,0:T(8,128)S(1)} %convolution_bitcast_fusion.8), channel_id=3, replica_groups=mesh['gx'=8,'gy'=4] {'gx','gy'}, dimensions={0}, use_global_device_ids=true | all-gather | bytes 135168 | tf_op jit(solution)/shard_map/all_gather | solution.py:11
  562.2 2.9 cholesky.230
  568.0 4.5 collective-permute-start.25
  573.2 3.1 custom-call.23
  579.7 39.3 %all-reduce.19 = (f32[32,32]{0,1:T(8,128)S(1)}, f32[32,32]{1,0:T(8,128)S(1)}) all-reduce(f32[32,32]{0,1:T(8,128)S(1)} %convolution_bitcast_fusion.9, f32[32,32]{1,0:T(8,128)S(1)} %convolution_bitcast_fusion.7), channel_id=1, replica_groups=mesh['gx'=8,'gy'=4] {'gx','gy'}, use_global_device_ids=true, to_apply=%region_16.19 | all-reduce | flops 2048 | bytes 16384 | tf_op jit(solution)/shard_map/psum | solution.py:134
  619.1 2.9 cholesky.219
  631.0 2.9 cholesky.252
  635.3 3.0 collective-permute-start.27
  642.4 4.7 collective-permute-start.29
  647.7 3.1 custom-call.25
  654.9 44.3 %all-reduce.18 = (f32[32,32]{0,1:T(8,128)S(1)}, f32[32,32]{1,0:T(8,128)S(1)}, f32[32,32]{1,0:T(8,128)S(1)}) all-reduce(f32[32,32]{0,1:T(8,128)S(1)} %convolution_bitcast_fusion.5, f32[32,32]{1,0:T(8,128)S(1)} %convolution_bitcast_fusion.3, f32[32,32]{1,0:T(8,128)S(1)} %convolution_bitcast_fusion.4), channel_id=1, replica_groups=mesh['gx'=8,'gy'=4] {'gx','gy'}, use_global_device_ids=true, to_apply=%region_19.22 | all-reduce | flops 3072 | bytes 24576 | tf_op jit(solution)/shard_map/psum | solution.py:134
  699.3 2.9 cholesky.241
  709.9 3.0 collective-permute-start.31
  716.1 4.5 collective-permute-start.33
  724.8 44.2 %psum.101 = f32[32,32]{0,1:T(8,128)S(1)} all-reduce(f32[32,32]{0,1:T(8,128)S(1)} %convolution_bitcast_fusion.1), channel_id=1, replica_groups=mesh['gx'=8,'gy'=4] {'gx','gy'}, use_global_device_ids=true, to_apply=%region_22.25 | all-reduce | flops 1024 | bytes 8192 | tf_op jit(solution)/shard_map/psum | solution.py:134
  769.0 2.9 cholesky.263
  (364 shorter events, 138.7 us)
Async XLA Ops:
  0.6 12.1 %copy-start = (f32[64,64]{1,0:T(8,128)S(1)}, f32[64,64]{1,0:T(8,128)}, u32[]{:S(2)}) copy-start(f32[64,64]{1,0:T(8,128)} %param.24) | copy-start | bytes 49156
  0.6 11.6 %copy-start.14 = (s32[8192,1]{0,1:T(1,128)S(1)}, s32[8192,1]{0,1:T(1,128)}, u32[]{:S(2)}) copy-start(s32[8192,1]{0,1:T(1,128)} %param.25) | copy-start | bytes 98308
  1.6 11.1 %copy-start.35 = (f32[8192]{0:T(1024)S(1)}, f32[8192]{0:T(1024)}, u32[]{:S(2)}) copy-start(f32[8192]{0:T(1024)} %param.28) | copy-start | bytes 98308
  1.6 11.1 %copy-start.36 = (s32[8192]{0:T(1024)S(1)}, s32[8192]{0:T(1024)}, u32[]{:S(2)}) copy-start(s32[8192]{0:T(1024)} %param.27) | copy-start | bytes 98308
  43.3 7.4 copy-start.2
  43.3 11.8 %copy-start.9 = (f32[4,8,128]{2,1,0:T(8,128)S(1)}, f32[4,8,128]{2,1,0:T(8,128)}, u32[]{:S(2)}) copy-start(f32[4,8,128]{2,1,0:T(8,128)} %param.22) | copy-start | bytes 49156
  43.3 15.4 %copy-start.10 = (f32[4,8,128]{2,1,0:T(8,128)S(1)}, f32[4,8,128]{2,1,0:T(8,128)}, u32[]{:S(2)}) copy-start(f32[4,8,128]{2,1,0:T(8,128)} %param.21) | copy-start | bytes 49156
  43.3 19.2 %copy-start.33 = (s32[2]{0:T(128)S(1)}, s32[2]{0:T(128)}, u32[]{:S(2)}) copy-start(s32[2]{0:T(128)} %constant.171) | copy-start | bytes 28
  43.3 19.3 %copy-start.34 = (s32[2]{0:T(128)S(1)}, s32[2]{0:T(128)}, u32[]{:S(2)}) copy-start(s32[2]{0:T(128)} %constant.174) | copy-start | bytes 28
  43.3 54.2 %all-to-all-start = ((bf16[64,32,512]{2,0,1:T(8,128)(2,1)}), bf16[64,32,512]{2,0,1:T(8,128)(2,1)S(1)}, u32[]{:S(2)}, u32[]{:S(2)}) async-start(bf16[64,32,512]{2,0,1:T(8,128)(2,1)} %copy.216), calls=%async_computation | async-start | bytes 4194304 | tf_op jit(solution)/shard_map/all_to_all | solution.py:97
  50.7 44.4 %slice-start = ((f32[4,8,128]{2,1,0:T(8,128)}), f32[3,8,128]{2,1,0:T(8,128)S(1)}, s32[]{:S(2)}) async-start(f32[4,8,128]{2,1,0:T(8,128)} %param.23), calls=%async_computation.2 | async-start | bytes 24576 | tf_op jit(solution)/shard_map/slice | solution.py:118
  50.7 44.5 %copy-start.8 = (f32[4,8,128]{2,1,0:T(8,128)S(1)}, f32[4,8,128]{2,1,0:T(8,128)}, u32[]{:S(2)}) copy-start(f32[4,8,128]{2,1,0:T(8,128)} %param.20) | copy-start | bytes 49156
  51.7 43.5 %collective-permute-start.2 = (f32[32,4,1,128]{3,0,2,1:T(8,128)S(1)}, f32[32,4,1,128]{3,0,2,1:T(8,128)S(1)}, u32[]{:S(2)}, u32[]{:S(2)}) collective-permute-start(f32[32,4,1,128]{3,0,2,1:T(8,128)S(1)} %get-tuple-element.213), channel_id=1, source_target_pairs={{0,4},{4,8},{8,12},{12,16},{16,20},{20,24},{24,28},{1,5},{5,9},{9,... | collective-permute-start | bytes 196616 | tf_op jit(solution)/shard_map/ppermute | solution.py:24
  53.8 43.6 %collective-permute-start = (f32[32,4,1,128]{3,0,2,1:T(8,128)}, f32[32,4,1,128]{3,0,2,1:T(8,128)S(1)}, u32[]{:S(2)}, u32[]{:S(2)}) collective-permute-start(f32[32,4,1,128]{3,0,2,1:T(8,128)} %get-tuple-element.212), channel_id=1, source_target_pairs={{4,0},{8,4},{12,8},{16,12},{20,16},{24,20},{28,24},{5,1},{9,5},{13... | collective-permute-start | bytes 196616 | tf_op jit(solution)/shard_map/ppermute | solution.py:27
  55.2 39.9 %collective-permute-start.4 = (f32[4,8,1]{2,1,0:T(8,128)S(1)}, f32[4,8,1]{2,1,0:T(8,128)S(1)}, u32[]{:S(2)}, u32[]{:S(2)}) collective-permute-start(f32[4,8,1]{2,1,0:T(8,128)S(1)} %slice.379), channel_id=1, source_target_pairs={{0,1},{1,2},{2,3},{4,5},{5,6},{6,7},{8,9},{9,10},{10,11},{12,13},{... | collective-permute-start | bytes 392 | tf_op jit(solution)/shard_map/ppermute | solution.py:35
  58.8 56.2 %collective-permute-start.1 = (f32[4,1,128]{2,1,0:T(1,128)S(1)}, f32[4,1,128]{2,1,0:T(1,128)S(1)}, u32[]{:S(2)}, u32[]{:S(2)}) collective-permute-start(f32[4,1,128]{2,1,0:T(1,128)S(1)} %slice.373), channel_id=1, source_target_pairs={{0,4},{4,8},{8,12},{12,16},{16,20},{20,24},{24,28},{1,5},{5,9},{9,... | collective-permute-start | bytes 6152 | tf_op jit(solution)/shard_map/ppermute | solution.py:35
  95.2 10.9 %copy-start.17 = (f32[32,4,1,128]{3,0,2,1:T(8,128)}, f32[32,4,1,128]{3,0,2,1:T(8,128)S(1)}, u32[]{:S(2)}) copy-start(f32[32,4,1,128]{3,0,2,1:T(8,128)S(1)} %collective-permute-done.2) | copy-start | bytes 196612
  97.4 12.8 %copy-start.18 = (f32[32,4,1,128]{3,0,2,1:T(8,128)}, f32[32,4,1,128]{3,0,2,1:T(8,128)S(1)}, u32[]{:S(2)}) copy-start(f32[32,4,1,128]{3,0,2,1:T(8,128)S(1)} %collective-permute-done) | copy-start | bytes 196612
  97.6 21.4 %all-to-all-start.1 = ((s32[1,32,512]{2,0,1:T(1,128)}), s32[1,32,512]{2,0,1:T(1,128)}, u32[]{:S(2)}, u32[]{:S(2)}) async-start(s32[1,32,512]{2,0,1:T(1,128)} %bitcast.352), calls=%async_computation.1 | async-start | bytes 131072 | tf_op jit(solution)/shard_map/all_to_all | solution.py:98
  107.5 7.4 collective-permute-start.3
  110.2 6.0 collective-permute-start.5
  118.9 55.5 %copy-start.4 = (f32[32,4,8,128]{3,0,2,1:T(8,128)S(1)}, f32[32,4,8,128]{3,0,2,1:T(8,128)}, u32[]{:S(2)}) copy-start(f32[32,4,8,128]{3,0,2,1:T(8,128)} %get-tuple-element.215) | copy-start | bytes 1572868
  118.9 55.6 %copy-start.5 = (f32[32,4,10,1]{3,0,2,1:T(8,128)S(1)}, f32[32,4,10,1]{3,0,2,1:T(8,128)}, u32[]{:S(2)}) copy-start(f32[32,4,10,1]{3,0,2,1:T(8,128)} %copy.227) | copy-start | bytes 15364
  118.9 55.6 %copy-start.7 = (f32[32,3,8,128]{3,0,2,1:T(8,128)S(1)}, f32[32,3,8,128]{3,0,2,1:T(8,128)}, u32[]{:S(2)}) copy-start(f32[32,3,8,128]{3,0,2,1:T(8,128)} %get-tuple-element.210) | copy-start | bytes 1179652
  119.0 55.6 %copy-start.11 = (f32[4,8,128]{2,1,0:T(8,128)S(1)}, f32[4,8,128]{2,1,0:T(8,128)}, u32[]{:S(2)}) copy-start(f32[4,8,128]{2,1,0:T(8,128)} %param.23) | copy-start | bytes 49156
  177.1 80.8 %collective-permute-start.6 = (f32[32,4,1,128]{3,0,2,1:T(8,128)S(1)}, f32[32,4,1,128]{3,0,2,1:T(8,128)S(1)}, u32[]{:S(2)}, u32[]{:S(2)}) collective-permute-start(f32[32,4,1,128]{3,0,2,1:T(8,128)S(1)} %get-tuple-element.209), channel_id=1, source_target_pairs={{4,0},{8,4},{12,8},{16,12},{20,16},{24,20},{28,24},{5,1},{9,5},{13... | collective-permute-start | bytes 196616 | tf_op jit(solution)/shard_map/ppermute | solution.py:27
  178.4 79.5 %collective-permute-start.7 = (f32[32,4,1,128]{3,0,2,1:T(8,128)S(1)}, f32[32,4,1,128]{3,0,2,1:T(8,128)S(1)}, u32[]{:S(2)}, u32[]{:S(2)}) collective-permute-start(f32[32,4,1,128]{3,0,2,1:T(8,128)S(1)} %get-tuple-element.208), channel_id=1, source_target_pairs={{0,4},{4,8},{8,12},{12,16},{16,20},{20,24},{24,28},{1,5},{5,9},{9,... | collective-permute-start | bytes 196616 | tf_op jit(solution)/shard_map/ppermute | solution.py:24
  257.9 10.4 %copy-start.13 = (f32[4,8,8,128]{3,1,2,0:T(8,128)S(1)}, f32[4,8,8,128]{3,1,2,0:T(8,128)}, u32[]{:S(2)}) copy-start(f32[4,8,8,128]{3,1,2,0:T(8,128)} %get-tuple-element.216) | copy-start | bytes 393220
  258.5 10.6 %collective-permute-start.8 = (f32[32,4,10,1]{0,1,3,2:T(4,128)S(1)}, f32[32,4,10,1]{0,1,3,2:T(4,128)S(1)}, u32[]{:S(2)}, u32[]{:S(2)}) collective-permute-start(f32[32,4,10,1]{0,1,3,2:T(4,128)S(1)} %copy.236), channel_id=1, source_target_pairs={{1,0},{2,1},{3,2},{5,4},{6,5},{7,6},{9,8},{10,9},{11,10},{13,12},{... | collective-permute-start | bytes 15368 | tf_op jit(solution)/shard_map/ppermute | solution.py:27
  260.1 9.3 %collective-permute-start.9 = (f32[32,4,10,1]{0,1,3,2:T(4,128)S(1)}, f32[32,4,10,1]{0,1,3,2:T(4,128)S(1)}, u32[]{:S(2)}, u32[]{:S(2)}) collective-permute-start(f32[32,4,10,1]{0,1,3,2:T(4,128)S(1)} %copy.238), channel_id=1, source_target_pairs={{0,1},{1,2},{2,3},{4,5},{5,6},{6,7},{8,9},{9,10},{10,11},{12,13},{... | collective-permute-start | bytes 15368 | tf_op jit(solution)/shard_map/ppermute | solution.py:24
  270.4 48.2 %copy-start.29 = (f32[1,32,32]{1,2,0:T(8,128)S(1)}, f32[1,32,32]{1,2,0:T(8,128)}, u32[]{:S(2)}) copy-start(f32[1,32,32]{1,2,0:T(8,128)} %custom-call.18) | copy-start | bytes 12292
  318.1 2.5 copy-start.3
  324.4 5.1 collective-permute-start.10
  325.7 3.9 collective-permute-start.11
  331.3 10.1 %collective-permute-start.12 = (f32[32,4,10,1]{0,1,3,2:T(4,128)S(1)}, f32[32,4,10,1]{0,1,3,2:T(4,128)S(1)}, u32[]{:S(2)}, u32[]{:S(2)}) collective-permute-start(f32[32,4,10,1]{0,1,3,2:T(4,128)S(1)} %copy.250), channel_id=1, source_target_pairs={{1,0},{2,1},{3,2},{5,4},{6,5},{7,6},{9,8},{10,9},{11,10},{13,12},{... | collective-permute-start | bytes 15368 | tf_op jit(solution)/shard_map/ppermute | solution.py:27
  332.9 8.9 %collective-permute-start.13 = (f32[32,4,10,1]{0,1,3,2:T(4,128)S(1)}, f32[32,4,10,1]{0,1,3,2:T(4,128)S(1)}, u32[]{:S(2)}, u32[]{:S(2)}) collective-permute-start(f32[32,4,10,1]{0,1,3,2:T(4,128)S(1)} %copy.252), channel_id=1, source_target_pairs={{0,1},{1,2},{2,3},{4,5},{5,6},{6,7},{8,9},{9,10},{10,11},{12,13},{... | collective-permute-start | bytes 15368 | tf_op jit(solution)/shard_map/ppermute | solution.py:24
  344.5 53.8 %copy-start.30 = (f32[1,32,32]{1,2,0:T(8,128)S(1)}, f32[1,32,32]{1,2,0:T(8,128)}, u32[]{:S(2)}) copy-start(f32[1,32,32]{1,2,0:T(8,128)} %custom-call.20) | copy-start | bytes 12292
  399.3 5.0 collective-permute-start.14
  400.6 3.9 collective-permute-start.15
  405.8 8.3 %copy-start.26 = (f32[32,4,1,128]{3,0,2,1:T(8,128)S(1)}, f32[32,4,1,128]{3,0,2,1:T(8,128)}, u32[]{:S(2)}) copy-start(f32[32,4,1,128]{3,0,2,1:T(8,128)} %copy-done.25) | copy-start | bytes 196612
  405.9 8.3 %copy-start.28 = (f32[32,4,1,128]{3,0,2,1:T(8,128)S(1)}, f32[32,4,1,128]{3,0,2,1:T(8,128)}, u32[]{:S(2)}) copy-start(f32[32,4,1,128]{3,0,2,1:T(8,128)} %copy-done.27) | copy-start | bytes 196612
  406.2 6.3 collective-permute-start.16
  407.8 6.0 collective-permute-start.17
  466.7 5.2 collective-permute-start.18
  468.0 3.9 collective-permute-start.19
  473.2 7.1 copy-start.12
  473.8 6.6 collective-permute-start.20
  475.4 6.0 collective-permute-start.21
  484.9 80.9 %collective-permute-start.22 = (f32[32,4,1,128]{3,0,2,1:T(8,128)S(1)}, f32[32,4,1,128]{3,0,2,1:T(8,128)S(1)}, u32[]{:S(2)}, u32[]{:S(2)}) collective-permute-start(f32[32,4,1,128]{3,0,2,1:T(8,128)S(1)} %get-tuple-element.193), channel_id=1, source_target_pairs={{4,0},{8,4},{12,8},{16,12},{20,16},{24,20},{28,24},{5,1},{9,5},{13... | collective-permute-start | bytes 196616 | tf_op jit(solution)/shard_map/ppermute | solution.py:27
  486.2 79.6 %collective-permute-start.23 = (f32[32,4,1,128]{3,0,2,1:T(8,128)S(1)}, f32[32,4,1,128]{3,0,2,1:T(8,128)S(1)}, u32[]{:S(2)}, u32[]{:S(2)}) collective-permute-start(f32[32,4,1,128]{3,0,2,1:T(8,128)S(1)} %get-tuple-element.192), channel_id=1, source_target_pairs={{0,4},{4,8},{8,12},{12,16},{16,20},{20,24},{24,28},{1,5},{5,9},{9,... | collective-permute-start | bytes 196616 | tf_op jit(solution)/shard_map/ppermute | solution.py:24
  566.4 9.9 %collective-permute-start.24 = (f32[32,4,10,1]{0,1,3,2:T(4,128)S(1)}, f32[32,4,10,1]{0,1,3,2:T(4,128)S(1)}, u32[]{:S(2)}, u32[]{:S(2)}) collective-permute-start(f32[32,4,10,1]{0,1,3,2:T(4,128)S(1)} %copy.274), channel_id=1, source_target_pairs={{1,0},{2,1},{3,2},{5,4},{6,5},{7,6},{9,8},{10,9},{11,10},{13,12},{... | collective-permute-start | bytes 15368 | tf_op jit(solution)/shard_map/ppermute | solution.py:27
  568.0 8.6 %collective-permute-start.25 = (f32[32,4,10,1]{0,1,3,2:T(4,128)S(1)}, f32[32,4,10,1]{0,1,3,2:T(4,128)S(1)}, u32[]{:S(2)}, u32[]{:S(2)}) collective-permute-start(f32[32,4,10,1]{0,1,3,2:T(4,128)S(1)} %copy.276), channel_id=1, source_target_pairs={{0,1},{1,2},{2,3},{4,5},{5,6},{6,7},{8,9},{9,10},{10,11},{12,13},{... | collective-permute-start | bytes 15368 | tf_op jit(solution)/shard_map/ppermute | solution.py:24
  578.5 49.0 %copy-start.32 = (f32[1,32,32]{1,2,0:T(8,128)S(1)}, f32[1,32,32]{1,2,0:T(8,128)}, u32[]{:S(2)}) copy-start(f32[1,32,32]{1,2,0:T(8,128)} %custom-call.23) | copy-start | bytes 12292
  634.0 5.0 collective-permute-start.26
  635.3 3.9 collective-permute-start.27
  640.8 10.0 %collective-permute-start.28 = (f32[32,4,10,1]{0,1,3,2:T(4,128)S(1)}, f32[32,4,10,1]{0,1,3,2:T(4,128)S(1)}, u32[]{:S(2)}, u32[]{:S(2)}) collective-permute-start(f32[32,4,10,1]{0,1,3,2:T(4,128)S(1)} %copy.287), channel_id=1, source_target_pairs={{1,0},{2,1},{3,2},{5,4},{6,5},{7,6},{9,8},{10,9},{11,10},{13,12},{... | collective-permute-start | bytes 15368 | tf_op jit(solution)/shard_map/ppermute | solution.py:27
  642.4 8.7 %collective-permute-start.29 = (f32[32,4,10,1]{0,1,3,2:T(4,128)S(1)}, f32[32,4,10,1]{0,1,3,2:T(4,128)S(1)}, u32[]{:S(2)}, u32[]{:S(2)}) collective-permute-start(f32[32,4,10,1]{0,1,3,2:T(4,128)S(1)} %copy.289), channel_id=1, source_target_pairs={{0,1},{1,2},{2,3},{4,5},{5,6},{6,7},{8,9},{9,10},{10,11},{12,13},{... | collective-permute-start | bytes 15368 | tf_op jit(solution)/shard_map/ppermute | solution.py:24
  653.7 53.9 %copy-start.31 = (f32[1,32,32]{1,2,0:T(8,128)S(1)}, f32[1,32,32]{1,2,0:T(8,128)}, u32[]{:S(2)}) copy-start(f32[1,32,32]{1,2,0:T(8,128)} %custom-call.25) | copy-start | bytes 12292
  654.9 58.1 %copy-start.6 = (f32[32,4,8,128]{3,0,2,1:T(8,128)S(1)}, f32[32,4,8,128]{3,0,2,1:T(8,128)}, u32[]{:S(2)}) copy-start(f32[32,4,8,128]{3,0,2,1:T(8,128)} %convolution_add_fusion.4) | copy-start | bytes 1572868
  708.6 5.0 collective-permute-start.30
  709.9 3.9 collective-permute-start.31
  714.5 7.1 collective-permute-start.32
  716.1 6.0 collective-permute-start.33
  776.2 3.4 copy-start.1
  (10 other events, 6.4 us)
